TPU v7x, 32 devices: a whole 2x2x4 slice. The times are simulated.
32 devices in a mesh: rep: 8 (over y, x, core), tp: 4 (over z).
Axes of the slice: x: 2, y: 2, z: 4, core: 2. Of those that a mesh axis runs over, the one named last changes fastest.
Arguments:
- states: bfloat16 [4, 32, 8192], P(None, 'rep'), may hold values from -6 to 6
- norm_gain: float32 [8192], replicated, may hold values from 0.1 to 1.9
- w_query: bfloat16 [8192, 8192], P(('rep', 'tp')), may hold values from -0.0625 to 0.0625
- w_key: bfloat16 [8192, 1024], P(('rep', 'tp')), may hold values from -0.0625 to 0.0625
- w_value: bfloat16 [8192, 1024], P(('rep', 'tp')), may hold values from -0.0625 to 0.0625
- w_out: bfloat16 [8192, 8192], P(None, ('rep', 'tp')), may hold values from -0.0625 to 0.0625
- bias_query: bfloat16 [8192], P('tp'), may hold values from -4 to 4
- bias_key: bfloat16 [1024], P('tp'), may hold values from -4 to 4
- bias_value: bfloat16 [1024], P('tp'), may hold values from -4 to 4
- key_cache: bfloat16 [32, 8, 4096, 128], P('rep', 'tp'), may hold values from -120 to 120
- value_cache: bfloat16 [32, 8, 4096, 128], P('rep', 'tp'), may hold values from -6 to 6
- lengths: int32 [32], P('rep'), may hold values from 1 to 4096, as said below
Outputs:
- mixed: bfloat16 [4, 32, 8192], P(None, 'rep', 'tp')
Inputs may be any that keep to these rules, and one draw needn't show every extreme that they name: `lengths`: each row's number of live cached positions; some row has exactly 4096.
All inputs are finite; a program needn't handle non-finite values.
Results may differ from a plain program's by a relative error of at most 0.0084.
Values may be sent and summed in bfloat16 or wider, within the bound.
A program may use at most 128 MiB of HBM per device.

v0:
```python
import jax
import jax.numpy as jnp
from jax import lax
from jax.sharding import PartitionSpec as P

BLK = 512
THETA = 1000000.0
EPS = 1e-06


def rotate(vectors, positions, head_size):
    half = head_size // 2
    freqs = THETA ** (-jnp.arange(half, dtype=jnp.float32) * 2.0 / head_size)
    angles = positions.astype(jnp.float32)[..., None, None] * freqs
    first = vectors[..., :half]
    second = vectors[..., half:]
    cosine = jnp.cos(angles)
    sine = jnp.sin(angles)
    return jnp.concatenate(
        [first * cosine - second * sine, second * cosine + first * sine], axis=-1
    )


def absorb(carry, scores, valid, values):
    top, total, accum = carry
    scores = jnp.where(valid, scores, -1e30)
    fresh = jnp.maximum(top, jnp.max(scores, axis=-1))
    weights = jnp.where(valid, jnp.exp(scores - fresh[..., None]), 0.0)
    factor = jnp.exp(top - fresh)
    total = total * factor + jnp.sum(weights, axis=-1)
    accum = accum * factor[..., None] + jnp.einsum(
        "bkqc,bkch->bkqh", weights.astype(jnp.bfloat16), values, preferred_element_type=jnp.float32
    )
    return (fresh, total, accum)


def attend(query, new_keys, new_values, key_cache, value_cache, lengths):
    steps, rows, heads_q, head_size = query.shape
    heads_kv = key_cache.shape[1]
    group = heads_q // heads_kv
    count = steps * group
    scale = 1.0 / head_size**0.5
    grouped = query.reshape(steps, rows, heads_kv, group, head_size).transpose(1, 2, 0, 3, 4)
    grouped = grouped.reshape(rows, heads_kv, count, head_size)
    start_top = jnp.full((rows, heads_kv, count), -1e30, jnp.float32)
    start_total = jnp.zeros((rows, heads_kv, count), jnp.float32)
    start_accum = jnp.zeros((rows, heads_kv, count, head_size), jnp.float32)

    def visit(index, carry):
        start = index * BLK
        keys = lax.dynamic_slice_in_dim(key_cache, start, BLK, 2)
        values = lax.dynamic_slice_in_dim(value_cache, start, BLK, 2)
        scores = (
            jnp.einsum("bkqh,bkch->bkqc", grouped, keys, preferred_element_type=jnp.float32) * scale
        )
        place = start + jnp.arange(BLK, dtype=jnp.int32)
        valid = (place[None, :] < lengths[:, None])[:, None, None, :]
        return absorb(carry, scores, valid, values)

    bound = key_cache.shape[2] // BLK
    carry = lax.fori_loop(0, bound, visit, (start_top, start_total, start_accum))
    fresh_keys = new_keys.transpose(1, 2, 0, 3)
    fresh_values = new_values.transpose(1, 2, 0, 3)
    scores = (
        jnp.einsum("bkqh,bkjh->bkqj", grouped, fresh_keys, preferred_element_type=jnp.float32)
        * scale
    )
    rank = jnp.arange(count, dtype=jnp.int32) // group
    valid = (jnp.arange(steps, dtype=jnp.int32)[None, :] <= rank[:, None])[None, None, :, :]
    top, total, accum = absorb(carry, scores, valid, fresh_values)
    attended = accum / total[..., None]
    attended = attended.reshape(rows, heads_kv, steps, group, head_size).transpose(2, 0, 1, 3, 4)
    return attended.reshape(steps * rows, heads_q * head_size).astype(jnp.bfloat16)


def on_device(
    states,
    norm_gain,
    w_query,
    w_key,
    w_value,
    w_out,
    bias_query,
    bias_key,
    bias_value,
    key_cache,
    value_cache,
    lengths,
):
    steps, rows, width = states.shape
    head_size = key_cache.shape[3]
    query_rows, key_rows, value_rows = (
        lax.all_to_all(w_query, "tp", split_axis=1, concat_axis=0, tiled=True),
        lax.all_to_all(w_key, "tp", split_axis=1, concat_axis=0, tiled=True),
        lax.all_to_all(w_value, "tp", split_axis=1, concat_axis=0, tiled=True),
    )
    out_block = lax.all_to_all(w_out, "tp", split_axis=0, concat_axis=1, tiled=True)
    flat = states.reshape(steps * rows, width).astype(jnp.float32)
    factor = lax.rsqrt(jnp.mean(flat * flat, axis=-1, keepdims=True) + EPS)
    normed = (flat * factor * norm_gain).astype(jnp.bfloat16)
    local_width = query_rows.shape[1]
    kv_width = key_rows.shape[1]
    stacked = jnp.concatenate([query_rows, key_rows, value_rows], axis=1)
    spread = lax.all_to_all(normed, "rep", split_axis=1, concat_axis=0, tiled=True)
    joined = lax.psum_scatter(
        jnp.dot(spread, stacked, preferred_element_type=jnp.float32),
        "rep",
        scatter_dimension=0,
        tiled=True,
    )
    query = joined[:, :local_width]
    keys = joined[:, local_width : local_width + kv_width]
    values = joined[:, local_width + kv_width :]
    query = query + bias_query.astype(jnp.float32)
    keys = keys + bias_key.astype(jnp.float32)
    values = values + bias_value.astype(jnp.float32)
    positions = lengths[None, :] + jnp.arange(steps, dtype=jnp.int32)[:, None]
    query = rotate(
        query.reshape(steps, rows, local_width // head_size, head_size), positions, head_size
    ).astype(jnp.bfloat16)
    keys = rotate(
        keys.reshape(steps, rows, kv_width // head_size, head_size), positions, head_size
    ).astype(jnp.bfloat16)
    values = values.reshape(steps, rows, kv_width // head_size, head_size).astype(jnp.bfloat16)
    attended = attend(query, keys, values, key_cache, value_cache, lengths)
    pieces = jnp.dot(
        lax.all_gather(attended, "rep", axis=0, tiled=True),
        out_block,
        preferred_element_type=jnp.float32,
    )
    partial_value = lax.all_to_all(
        pieces.astype(jnp.bfloat16), "rep", split_axis=0, concat_axis=1, tiled=True
    ).astype(pieces.dtype)
    summed = lax.psum_scatter(
        partial_value.astype(jnp.bfloat16), "tp", scatter_dimension=1, tiled=True
    ).astype(jnp.float32)
    column = lax.axis_index("tp") * summed.shape[1]
    residual = lax.dynamic_slice_in_dim(flat, column, summed.shape[1], 1)
    return (residual + summed).astype(jnp.bfloat16).reshape(steps, rows, summed.shape[1])


def solution(mesh):
    return jax.shard_map(
        on_device,
        mesh=mesh,
        in_specs=(
            P(None, "rep", None),
            P(),
            P(("rep", "tp"), None),
            P(("rep", "tp"), None),
            P(("rep", "tp"), None),
            P(None, ("rep", "tp")),
            P("tp"),
            P("tp"),
            P("tp"),
            P("rep", "tp", None, None),
            P("rep", "tp", None, None),
            P("rep"),
        ),
        out_specs=P(None, "rep", "tp"),
        check_vma=False,
    )
```

profile of v0, /device:TPU:0, one launch (start us, length us, event | category | flops | bytes accessed | tf_op | source)
XLA Modules:
  0.0 342.6 jit_solution(18113901410279301556)
XLA Ops:
  6.5 1.1 reshape.184
  7.7 1.2 multiply_reduce_fusion
  8.9 0.8 mul.177
  9.9 0.9 copy.46
  10.7 5.2 %all-to-all-start = ((bf16[16,8,1024]{2,0,1:T(8,128)(2,1)}), bf16[16,8,1024]{2,0,1:T(8,128)(2,1)S(1)}, u32[]{:S(2)}, u32[]{:S(2)}) async-start(bf16[16,8,1024]{2,0,1:T(8,128)(2,1)} %copy.46), calls=%async_computation | async-start | bytes 524288 | tf_op jit(solution)/shard_map/all_to_all | solution.py:104
  15.9 2.0 copy.51
  18.0 4.9 %all-to-all-done = bf16[16,8,1024]{2,0,1:T(8,128)(2,1)S(1)} async-done(((bf16[16,8,1024]{2,0,1:T(8,128)(2,1)}), bf16[16,8,1024]{2,0,1:T(8,128)(2,1)S(1)}, u32[]{:S(2)}, u32[]{:S(2)}) %all-to-all-start) | async-done | bytes 262176 | tf_op jit(solution)/shard_map/all_to_all | solution.py:104
  22.8 4.9 %all-to-all-start.3 = ((bf16[256,4,256]{0,2,1:T(8,128)(2,1)}), bf16[256,4,256]{0,2,1:T(8,128)(2,1)S(1)}, u32[]{:S(2)}, u32[]{:S(2)}) async-start(bf16[256,4,256]{0,2,1:T(8,128)(2,1)} %bitcast.8), calls=%async_computation.3 | async-start | bytes 1048576 | tf_op jit(solution)/shard_map/all_to_all | solution.py:95
  27.7 1.0 copy.49
  28.7 12.9 %all-to-all-done.3 = bf16[256,4,256]{0,2,1:T(8,128)(2,1)S(1)} async-done(((bf16[256,4,256]{0,2,1:T(8,128)(2,1)}), bf16[256,4,256]{0,2,1:T(8,128)(2,1)S(1)}, u32[]{:S(2)}, u32[]{:S(2)}) %all-to-all-start.3) | async-done | bytes 524320 | tf_op jit(solution)/shard_map/all_to_all | solution.py:95
  41.6 3.5 %all-to-all-start.2 = ((bf16[256,4,256]{0,2,1:T(8,128)(2,1)}), bf16[256,4,256]{0,2,1:T(8,128)(2,1)S(1)}, u32[]{:S(2)}, u32[]{:S(2)}) async-start(bf16[256,4,256]{0,2,1:T(8,128)(2,1)} %bitcast.5), calls=%async_computation.2 | async-start | bytes 1048576 | tf_op jit(solution)/shard_map/all_to_all | solution.py:94
  45.1 6.4 %copy.47 = bf16[256,8192]{0,1:T(8,128)(2,1)} copy(bf16[256,8192]{1,0:T(8,128)(2,1)} %param.16) | data formatting | bytes 8388608 | tf_op args[2]
  51.5 7.6 %all-to-all-done.2 = bf16[256,4,256]{0,2,1:T(8,128)(2,1)S(1)} async-done(((bf16[256,4,256]{0,2,1:T(8,128)(2,1)}), bf16[256,4,256]{0,2,1:T(8,128)(2,1)S(1)}, u32[]{:S(2)}, u32[]{:S(2)}) %all-to-all-start.2) | async-done | bytes 524320 | tf_op jit(solution)/shard_map/all_to_all | solution.py:94
  59.1 98.4 %all_to_all.111 = bf16[256,4,2048]{0,2,1:T(8,128)(2,1)} all-to-all(bf16[256,4,2048]{0,2,1:T(8,128)(2,1)} %bitcast.65), channel_id=1, replica_groups=mesh['rep'=8,'tp'=4] {'tp'}, dimensions={1} | all-to-all | bytes 8388608 | tf_op jit(solution)/shard_map/all_to_all | solution.py:93
  157.5 4.8 %all-to-all-start.4 = ((bf16[4,2048,256]{2,1,0:T(8,128)(2,1)}), bf16[4,2048,256]{2,1,0:T(8,128)(2,1)}, u32[]{:S(2)}, u32[]{:S(2)}) async-start(bf16[4,2048,256]{2,1,0:T(8,128)(2,1)} %bitcast.66), calls=%async_computation.5 | async-start | bytes 8388608 | tf_op jit(solution)/shard_map/all_to_all | solution.py:97
  162.8 6.3 %copy.48 = bf16[4,256,2048]{2,1,0:T(8,128)(2,1)} copy(bf16[4,256,2048]{1,2,0:T(8,128)(2,1)} %bitcast.64) | data formatting | bytes 8388608 | tf_op jit(solution)/shard_map/all_to_all | solution.py:93
  169.1 4.2 %fusion.15 = f32[128,2560]{1,0:T(8,128)} fusion(bf16[128,1024]{1,0:T(8,128)(2,1)S(1)} %bitcast.77, bf16[1024,256]{1,0:T(8,128)(2,1)S(1)} %bitcast.75, bf16[1024,256]{1,0:T(8,128)(2,1)S(1)} %bitcast.76, bf16[1024,2048]{1,0:T(8,128)(2,1)} %bitcast.67), kind=kOutput, calls=%fused_computation.23 | convolution fusion | flops 686817280 | bytes 6815744 | tf_op jit(solution)/shard_map/dot_general | solution.py:106
  173.8 80.7 %all-to-all-done.4 = bf16[4,2048,256]{2,1,0:T(8,128)(2,1)} async-done(((bf16[4,2048,256]{2,1,0:T(8,128)(2,1)}), bf16[4,2048,256]{2,1,0:T(8,128)(2,1)}, u32[]{:S(2)}, u32[]{:S(2)}) %all-to-all-start.4) | async-done | bytes 4194336 | tf_op jit(solution)/shard_map/all_to_all | solution.py:97
  254.5 6.4 %copy.61 = bf16[2048,4,256]{0,2,1:T(8,128)(2,1)} copy(bf16[2048,4,256]{2,0,1:T(8,128)(2,1)} %bitcast.21) | data formatting | bytes 8388608 | tf_op jit(solution)/shard_map/all_to_all | solution.py:97
  260.9 0.7 fusion.28
  261.7 0.9 fusion.25
  262.9 29.9 %while.18 = (s32[]{:T(128)}, f32[4,2,32]{2,1,0:T(2,128)S(1)}, f32[4,2,32]{2,1,0:T(2,128)S(1)}, f32[4,2,32,128]{3,2,1,0:T(8,128)S(1)}, s32[4]{0:T(128)S(1)}, /*in...) while((s32[]{:T(128)}, f32[4,2,32]{2,1,0:T(2,128)S(1)}, ...), condition=%wide.region_5.6_spmd.clone, body=%wide.region_2.5_spmd.clone.sunk | while | flops 68390656 | bytes 4026571 | solution.py:61
  263.0 1.8 fusion.59
  264.8 0.2 fusion.61
  265.1 1.6 convolution_add_fusion.3
  266.7 1.8 fusion.59
  268.8 1.6 convolution_add_fusion.3
  270.5 1.8 fusion.59
  272.5 1.6 convolution_add_fusion.3
  274.2 1.8 fusion.59
  276.0 0.2 fusion.61
  276.3 1.6 convolution_add_fusion.3
  278.0 1.8 fusion.59
  280.0 1.6 convolution_add_fusion.3
  281.7 1.8 fusion.59
  283.7 1.6 convolution_add_fusion.3
  285.4 1.8 fusion.59
  287.5 1.6 convolution_add_fusion.3
  289.2 1.8 fusion.59
  291.2 1.6 convolution_add_fusion.3
  292.9 0.2 fusion.44
  293.4 9.5 %all_gather.3 = bf16[128,2048]{1,0:T(8,128)(2,1)S(1)} all-gather(bf16[16,2048]{1,0:T(8,128)(2,1)S(1)} %convert_element_type.94), channel_id=1, replica_groups=mesh['rep'=8,'tp'=4] {'rep'}, dimensions={0}, use_global_device_ids=true | all-gather | bytes 589824 | tf_op jit(solution)/shard_map/all_gather | solution.py:127
  303.0 3.7 %convolution_convert_fusion = bf16[128,1024]{1,0:T(8,128)(2,1)S(1)} fusion(bf16[128,2048]{1,0:T(8,128)(2,1)S(1)} %all_gather.3, bf16[2048,1024]{0,1:T(8,128)(2,1)} %bitcast.63), kind=kOutput, calls=%fused_computation.29 | convolution fusion | flops 537001984 | bytes 4980736 | tf_op jit(solution)/shard_map/dot_general | solution.py:126
  306.7 9.4 %all_to_all.112 = bf16[8,16,1024]{2,1,0:T(8,128)(2,1)S(1)} all-to-all(bf16[8,16,1024]{2,1,0:T(8,128)(2,1)S(1)} %bitcast.71), channel_id=1, replica_groups=mesh['rep'=8,'tp'=4] {'rep'}, dimensions={0} | all-to-all | bytes 524288 | tf_op jit(solution)/shard_map/all_to_all | solution.py:131
  316.1 0.7 copy.66
  316.9 17.3 %reduce-scatter.5.cloned.1.call-done = bf16[16,2048]{1,0:T(8,128)(2,1)} async-done(((bf16[16,8192]{1,0:T(8,128)(2,1)}), bf16[16,2048]{1,0:T(8,128)(2,1)}) %reduce-scatter.5.cloned.1.call-update) | async-done | bytes 65552 | tf_op jit(solution)/shard_map/reduce_scatter | solution.py:134
  334.2 0.9 add_convert_fusion
  335.1 0.7 reshape.182
  (95 shorter events, 4.0 us)
Async XLA Ops:
  6.5 21.2 %copy-start.1 = (bf16[256,1024]{1,0:T(8,128)(2,1)S(1)}, bf16[256,1024]{1,0:T(8,128)(2,1)}, u32[]{:S(2)}) copy-start(bf16[256,1024]{1,0:T(8,128)(2,1)} %param.17) | copy-start | bytes 1572868
  10.7 12.1 %all-to-all-start = ((bf16[16,8,1024]{2,0,1:T(8,128)(2,1)}), bf16[16,8,1024]{2,0,1:T(8,128)(2,1)S(1)}, u32[]{:S(2)}, u32[]{:S(2)}) async-start(bf16[16,8,1024]{2,0,1:T(8,128)(2,1)} %copy.46), calls=%async_computation | async-start | bytes 524288 | tf_op jit(solution)/shard_map/all_to_all | solution.py:104
  22.8 18.8 %all-to-all-start.3 = ((bf16[256,4,256]{0,2,1:T(8,128)(2,1)}), bf16[256,4,256]{0,2,1:T(8,128)(2,1)S(1)}, u32[]{:S(2)}, u32[]{:S(2)}) async-start(bf16[256,4,256]{0,2,1:T(8,128)(2,1)} %bitcast.8), calls=%async_computation.3 | async-start | bytes 1048576 | tf_op jit(solution)/shard_map/all_to_all | solution.py:95
  41.6 17.5 %all-to-all-start.2 = ((bf16[256,4,256]{0,2,1:T(8,128)(2,1)}), bf16[256,4,256]{0,2,1:T(8,128)(2,1)S(1)}, u32[]{:S(2)}, u32[]{:S(2)}) async-start(bf16[256,4,256]{0,2,1:T(8,128)(2,1)} %bitcast.5), calls=%async_computation.2 | async-start | bytes 1048576 | tf_op jit(solution)/shard_map/all_to_all | solution.py:94
  157.5 97.0 %all-to-all-start.4 = ((bf16[4,2048,256]{2,1,0:T(8,128)(2,1)}), bf16[4,2048,256]{2,1,0:T(8,128)(2,1)}, u32[]{:S(2)}, u32[]{:S(2)}) async-start(bf16[4,2048,256]{2,1,0:T(8,128)(2,1)} %bitcast.66), calls=%async_computation.5 | async-start | bytes 8388608 | tf_op jit(solution)/shard_map/all_to_all | solution.py:97
  162.3 98.6 %reduce-scatter.3.cloned.1.call-start = ((), (), s32[]{:S(2)}) async-start(), calls=%async_computation.8 | async-start | bytes 1474560 | tf_op jit(solution)/shard_map/reduce_scatter | solution.py:105
  169.1 4.3 %copy-start.4 = (bf16[256]{0:T(256)(128)(2,1)S(1)}, bf16[256]{0:T(256)(128)(2,1)}, u32[]{:S(2)}) copy-start(bf16[256]{0:T(256)(128)(2,1)} %param.21) | copy-start | bytes 1540
  169.1 4.4 %copy-start.5 = (bf16[256]{0:T(256)(128)(2,1)S(1)}, bf16[256]{0:T(256)(128)(2,1)}, u32[]{:S(2)}) copy-start(bf16[256]{0:T(256)(128)(2,1)} %param.22) | copy-start | bytes 1540
  169.1 4.4 %copy-start.2 = (s32[4]{0:T(128)S(1)}, s32[4]{0:T(128)}, u32[]{:S(2)}) copy-start(s32[4]{0:T(128)} %param.25) | copy-start | bytes 52
  169.1 4.6 %copy-start.3 = (bf16[2048]{0:T(1024)(128)(2,1)S(1)}, bf16[2048]{0:T(1024)(128)(2,1)}, u32[]{:S(2)}) copy-start(bf16[2048]{0:T(1024)(128)(2,1)} %param.20) | copy-start | bytes 12292
  173.4 160.9 %reduce-scatter.5.cloned.1.call-start = ((), (), s32[]{:S(2)}) async-start(), calls=%async_computation.9 | async-start | bytes 327680 | tf_op jit(solution)/shard_map/reduce_scatter | solution.py:134
  292.8 24.1 %copy-start = (bf16[4,4,8192]{2,1,0:T(4,128)(2,1)S(1)}, bf16[4,4,8192]{2,1,0:T(4,128)(2,1)}, u32[]{:S(2)}) copy-start(bf16[4,4,8192]{2,1,0:T(4,128)(2,1)} %param.14) | copy-start | bytes 786436
Sparse Core Ops, SparseCore 0:
  173.5 37.2 reduce-scatter.2
  317.0 17.1 reduce-scatter.4
where the time goes:
time: 344 us; the launch traced here: 343 us
  waiting for transfers between devices  123 us (36%)
  blocking collectives  117 us (34%)
  matrix products  35.1 us (10%)
  local copies, waits for them, and re-layouts  27 us (8%)
  starting transfers between devices  18.5 us (5%)
  between operations  13.7 us (4%)
  other arithmetic  7.12 us (2%)
    all_to_all x1, blocking collectives, on_device(): lax.all_to_all(w_query, 'tp', split_axis=1, concat_axis=0, tiled=True)  98.4 us
    all_to_all x1, waiting for transfers between devices, on_device(): lax.all_to_all(w_out, 'tp', split_axis=0, concat_axis=1, tiled=True)  80.7 us
    reduce_scatter x1, waiting for transfers between devices, on_device(): lax.psum_scatter(partial_value.astype(jnp.bfloat16), 'tp', scatter_dimens...  17.3 us
    dot_general x8, matrix products, visit(): jnp.einsum('bkqh,bkch->bkqc', grouped, keys, preferred_element_type=jnp.f...  14.1 us
    all_to_all x1, waiting for transfers between devices, on_device(): lax.all_to_all(w_value, 'tp', split_axis=1, concat_axis=0, tiled=True)  12.9 us
    dot_general x9, matrix products, absorb(): jnp.einsum('bkqc,bkch->bkqh', weights.astype(jnp.bfloat16), values, prefe...  12.8 us
    all_gather x1, blocking collectives, on_device(): lax.all_gather(attended, 'rep', axis=0, tiled=True)  9.51 us
    unnamed x16, local copies, waits for them, and re-layouts  9.48 us
  transfers between devices with their start and end apart: 6, of which 5 were waited for; matrix products, arithmetic and copies ran while one was open for 8% of the time, Pallas kernels for 0%

commit v1 on v0

--- a/solution.py
+++ b/solution.py
@@ -87,10 +87,34 @@
     value_cache,
     lengths,
 ):
+
+    def state_trees(local_values, on_dim, where_dim):
+        block_out = jax.lax.axis_size("tp")
+        w_next = jax.lax.axis_index("tp")
+        all_rows, w1 = (block_out, w_next)
+        base_arr = local_values.shape[on_dim] // all_rows
+        r_now = list(local_values.shape)
+        r_now[on_dim] = base_arr
+        known = r_now[where_dim]
+        r_now[where_dim] = known * all_rows
+        p_next = jnp.zeros(r_now, local_values.dtype)
+        for dd in range(all_rows):
+            piece_now = lax.dynamic_slice_in_dim(
+                local_values, (w1 ^ dd) * base_arr, base_arr, axis=on_dim
+            )
+            if dd:
+                piece_now = jax.lax.ppermute(
+                    piece_now, "tp", [(p, p ^ dd) for p in range(all_rows)]
+                )
+            p_next = lax.dynamic_update_slice_in_dim(
+                p_next, piece_now, (w1 ^ dd) * known, axis=where_dim
+            )
+        return p_next
+
     steps, rows, width = states.shape
     head_size = key_cache.shape[3]
     query_rows, key_rows, value_rows = (
-        lax.all_to_all(w_query, "tp", split_axis=1, concat_axis=0, tiled=True),
+        state_trees(w_query, 1, 0),
         lax.all_to_all(w_key, "tp", split_axis=1, concat_axis=0, tiled=True),
         lax.all_to_all(w_value, "tp", split_axis=1, concat_axis=0, tiled=True),
     )

time: 344 us -> 282 us (0.82)
  blocking collectives: 117 us -> 20.2 us
  waiting for transfers between devices: 123 us -> 143 us
  starting transfers between devices: 18.5 us -> 36.7 us
    all_to_all x1 -> x0, blocking collectives: 98.4 us -> none  [on_device(): lax.all_to_all(w_query, 'tp', split_axis=1, concat_axis=0, tiled=True)]
    all_to_all x1, waiting for transfers between devices: 80.7 us -> 17.4 us  [on_device(): lax.all_to_all(w_out, 'tp', split_axis=0, concat_axis=1, tiled=True)]
    all_to_all x1, waiting for transfers between devices: 12.9 us -> 69.7 us  [on_device(): lax.all_to_all(w_value, 'tp', split_axis=1, concat_axis=0, tiled=True)]
    reduce_scatter x1, waiting for transfers between devices: 0.01 us -> 33.1 us  [on_device(): lax.psum_scatter(jnp.dot(spread, stacked, preferred_element_type=jnp.floa...]
    all_to_all x1, starting transfers between devices: 4.83 us -> 15 us  [on_device(): lax.all_to_all(w_out, 'tp', split_axis=0, concat_axis=1, tiled=True)]
    ppermute x0 -> x3, starting transfers between devices: none -> 8.17 us  [state_trees(): jax.lax.ppermute(piece_now, 'tp', [(p, p ^ dd) for p in range(all_rows)])]
    dynamic_update_slice x0 -> x3, local copies, waits for them, and re-layouts: none -> 6.98 us  [state_trees(): lax.dynamic_update_slice_in_dim(p_next, piece_now, (w1 ^ dd) * known, axi...]
    all_to_all x1 -> x0, local copies, waits for them, and re-layouts: 6.31 us -> none  [on_device(): lax.all_to_all(w_query, 'tp', split_axis=1, concat_axis=0, tiled=True)]
  transfers between devices with their start and end apart: 6 -> 9, of which waited for: 5 -> 5; matrix products, arithmetic and copies ran while one was open for 8% -> 16% of each run, Pallas kernels for 0% -> 0%
where the time goes in v1:
time: 282 us; the launch traced here: 281 us
  waiting for transfers between devices  143 us (51%)
  starting transfers between devices  36.7 us (13%)
  matrix products  35 us (12%)
  local copies, waits for them, and re-layouts  25.6 us (9%)
  blocking collectives  20.2 us (7%)
  between operations  13.7 us (5%)
  other arithmetic  6.17 us (2%)
    all_to_all x1, waiting for transfers between devices, on_device(): lax.all_to_all(w_value, 'tp', split_axis=1, concat_axis=0, tiled=True)  69.7 us
    reduce_scatter x1, waiting for transfers between devices, on_device(): lax.psum_scatter(jnp.dot(spread, stacked, preferred_element_type=jnp.floa...  33.1 us
    reduce_scatter x1, waiting for transfers between devices, on_device(): lax.psum_scatter(partial_value.astype(jnp.bfloat16), 'tp', scatter_dimens...  18.6 us
    all_to_all x1, waiting for transfers between devices, on_device(): lax.all_to_all(w_out, 'tp', split_axis=0, concat_axis=1, tiled=True)  17.4 us
    all_to_all x1, starting transfers between devices, on_device(): lax.all_to_all(w_out, 'tp', split_axis=0, concat_axis=1, tiled=True)  15 us
    dot_general x8, matrix products, visit(): jnp.einsum('bkqh,bkch->bkqc', grouped, keys, preferred_element_type=jnp.f...  14.1 us
    dot_general x9, matrix products, absorb(): jnp.einsum('bkqc,bkch->bkqh', weights.astype(jnp.bfloat16), values, prefe...  12.8 us
    all_to_all x1, blocking collectives, on_device(): lax.all_to_all(pieces.astype(jnp.bfloat16), 'rep', split_axis=0, concat_a...  10.4 us
  transfers between devices with their start and end apart: 9, of which 5 were waited for; matrix products, arithmetic and copies ran while one was open for 16% of the time, Pallas kernels for 0%

profile of v1, /device:TPU:0, one launch (start us, length us, event | category | flops | bytes accessed | tf_op | source)
XLA Modules:
  0.0 280.7 jit_solution(8963953840081262903)
XLA Ops:
  6.5 2.1 copy.45
  8.6 6.3 %all-to-all-start.1 = ((bf16[256,4,256]{0,2,1:T(8,128)(2,1)}), bf16[256,4,256]{0,2,1:T(8,128)(2,1)S(1)}, u32[]{:S(2)}, u32[]{:S(2)}) async-start(bf16[256,4,256]{0,2,1:T(8,128)(2,1)} %bitcast.2), calls=%async_computation.1 | async-start | bytes 1048576 | tf_op jit(solution)/shard_map/all_to_all | solution.py:118
  15.5 1.7 copy-done
  17.1 1.9 constant_dynamic-slice_fusion
  19.1 2.0 copy-done.1
  21.0 2.0 collective-permute-start
  23.1 2.4 collective-permute-start.1
  25.4 1.0 copy.47
  26.4 4.0 %all-to-all-done.1 = bf16[256,4,256]{0,2,1:T(8,128)(2,1)S(1)} async-done(((bf16[256,4,256]{0,2,1:T(8,128)(2,1)}), bf16[256,4,256]{0,2,1:T(8,128)(2,1)S(1)}, u32[]{:S(2)}, u32[]{:S(2)}) %all-to-all-start.1) | async-done | bytes 524320 | tf_op jit(solution)/shard_map/all_to_all | solution.py:118
  30.4 3.5 %all-to-all-start.2 = ((bf16[256,4,256]{0,2,1:T(8,128)(2,1)}), bf16[256,4,256]{0,2,1:T(8,128)(2,1)S(1)}, u32[]{:S(2)}, u32[]{:S(2)}) async-start(bf16[256,4,256]{0,2,1:T(8,128)(2,1)} %bitcast.5), calls=%async_computation.2 | async-start | bytes 1048576 | tf_op jit(solution)/shard_map/all_to_all | solution.py:119
  33.9 3.8 %collective-permute-start.2 = (bf16[256,2048]{1,0:T(8,128)(2,1)S(1)}, bf16[256,2048]{1,0:T(8,128)(2,1)}, u32[]{:S(2)}, u32[]{:S(2)}) collective-permute-start(bf16[256,2048]{1,0:T(8,128)(2,1)S(1)} %get-tuple-element.198), channel_id=1, source_target_pairs={{0,3},{1,2},{2,1},{3,0},{4,7},{5,6},{6,5},{7,4},{8,11},{9,10},{10,... | collective-permute-start | bytes 3145736 | tf_op jit(solution)/shard_map/ppermute | solution.py:106
  38.3 0.9 copy.44
  39.4 69.7 %all-to-all-done.2 = bf16[256,4,256]{0,2,1:T(8,128)(2,1)S(1)} async-done(((bf16[256,4,256]{0,2,1:T(8,128)(2,1)}), bf16[256,4,256]{0,2,1:T(8,128)(2,1)S(1)}, u32[]{:S(2)}, u32[]{:S(2)}) %all-to-all-start.2) | async-done | bytes 524320 | tf_op jit(solution)/shard_map/all_to_all | solution.py:119
  109.1 3.7 %all-to-all-start = ((bf16[16,8,1024]{2,0,1:T(8,128)(2,1)}), bf16[16,8,1024]{2,0,1:T(8,128)(2,1)S(1)}, u32[]{:S(2)}, u32[]{:S(2)}) async-start(bf16[16,8,1024]{2,0,1:T(8,128)(2,1)} %copy.44), calls=%async_computation | async-start | bytes 524288 | tf_op jit(solution)/shard_map/all_to_all | solution.py:128
  113.1 2.3 constant_dynamic-update-slice_fusion.2
  115.4 2.3 constant_dynamic-update-slice_fusion.1
  117.7 2.3 constant_dynamic-update-slice_fusion
  120.0 4.1 %fusion.15 = f32[128,2560]{1,0:T(8,128)} fusion(bf16[128,1024]{1,0:T(8,128)(2,1)S(1)} %bitcast.71, bf16[1024,256]{1,0:T(8,128)(2,1)S(1)} %bitcast.70, bf16[1024,256]{1,0:T(8,128)(2,1)S(1)} %bitcast.69, bf16[1024,2048]{1,0:T(8,128)(2,1)} %constant_dynamic-update-slice_fusion), kind=kOutput, calls=%fused_computation.23 | convolution fusion | flops 686817280 | bytes 6815744 | tf_op jit(solution)/shard_map/dot_general | solution.py:130
  124.3 15.0 %all-to-all-start.3 = ((bf16[4,2048,256]{2,1,0:T(8,128)(2,1)}), bf16[4,2048,256]{2,1,0:T(8,128)(2,1)}, u32[]{:S(2)}, u32[]{:S(2)}) async-start(bf16[4,2048,256]{2,1,0:T(8,128)(2,1)} %bitcast.61), calls=%async_computation.4 | async-start | bytes 8388608 | tf_op jit(solution)/shard_map/all_to_all | solution.py:121
  139.6 33.1 %reduce-scatter.3.cloned.1.call-done = f32[16,2560]{1,0:T(8,128)} async-done(((f32[128,2560]{1,0:T(8,128)}), f32[16,2560]{1,0:T(8,128)}) %reduce-scatter.3.cloned.1.call-update) | async-done | bytes 163856 | tf_op jit(solution)/shard_map/reduce_scatter | solution.py:129
  172.7 0.9 fusion.25
  173.9 29.9 %while.18 = (s32[]{:T(128)}, f32[4,2,32]{2,1,0:T(2,128)S(1)}, f32[4,2,32]{2,1,0:T(2,128)S(1)}, f32[4,2,32,128]{3,2,1,0:T(8,128)S(1)}, s32[4]{0:T(128)S(1)}, /*in...) while((s32[]{:T(128)}, f32[4,2,32]{2,1,0:T(2,128)S(1)}, ...), condition=%wide.region_5.6_spmd.clone, body=%wide.region_2.5_spmd.clone.sunk | while | flops 68390656 | bytes 4026571 | solution.py:61
  174.0 1.8 fusion.59
  176.0 1.6 convolution_add_fusion.3
  177.7 1.8 fusion.59
  179.8 1.6 convolution_add_fusion.3
  181.4 1.8 fusion.59
  183.5 1.6 convolution_add_fusion.3
  185.2 1.8 fusion.59
  187.2 1.6 convolution_add_fusion.3
  188.9 1.8 fusion.59
  191.0 1.6 convolution_add_fusion.3
  192.7 1.8 fusion.59
  194.7 1.6 convolution_add_fusion.3
  196.4 1.8 fusion.59
  198.4 1.6 convolution_add_fusion.3
  200.1 1.8 fusion.59
  202.2 1.6 convolution_add_fusion.3
  203.8 0.7 fusion.28
  205.2 9.8 %all_gather.3 = bf16[128,2048]{1,0:T(8,128)(2,1)S(1)} all-gather(bf16[16,2048]{1,0:T(8,128)(2,1)S(1)} %convert_element_type.94), channel_id=1, replica_groups=mesh['rep'=8,'tp'=4] {'rep'}, dimensions={0}, use_global_device_ids=true | all-gather | bytes 589824 | tf_op jit(solution)/shard_map/all_gather | solution.py:151
  215.1 17.4 %all-to-all-done.3 = bf16[4,2048,256]{2,1,0:T(8,128)(2,1)} async-done(((bf16[4,2048,256]{2,1,0:T(8,128)(2,1)}), bf16[4,2048,256]{2,1,0:T(8,128)(2,1)}, u32[]{:S(2)}, u32[]{:S(2)}) %all-to-all-start.3) | async-done | bytes 4194336 | tf_op jit(solution)/shard_map/all_to_all | solution.py:121
  232.5 6.3 %copy.57 = bf16[2048,4,256]{0,2,1:T(8,128)(2,1)} copy(bf16[2048,4,256]{2,0,1:T(8,128)(2,1)} %bitcast.18) | data formatting | bytes 8388608 | tf_op jit(solution)/shard_map/all_to_all | solution.py:121
  238.8 3.7 %convolution_convert_fusion = bf16[128,1024]{1,0:T(8,128)(2,1)S(1)} fusion(bf16[128,2048]{1,0:T(8,128)(2,1)S(1)} %all_gather.3, bf16[2048,1024]{0,1:T(8,128)(2,1)} %bitcast.60), kind=kOutput, calls=%fused_computation.29 | convolution fusion | flops 537001984 | bytes 4980736 | tf_op jit(solution)/shard_map/dot_general | solution.py:150
  242.5 10.4 %all_to_all.92 = bf16[8,16,1024]{2,1,0:T(8,128)(2,1)S(1)} all-to-all(bf16[8,16,1024]{2,1,0:T(8,128)(2,1)S(1)} %bitcast.65), channel_id=1, replica_groups=mesh['rep'=8,'tp'=4] {'rep'}, dimensions={0} | all-to-all | bytes 524288 | tf_op jit(solution)/shard_map/all_to_all | solution.py:155
  252.9 0.7 copy.62
  253.7 18.6 %reduce-scatter.5.cloned.1.call-done = bf16[16,2048]{1,0:T(8,128)(2,1)} async-done(((bf16[16,8192]{1,0:T(8,128)(2,1)}), bf16[16,2048]{1,0:T(8,128)(2,1)}) %reduce-scatter.5.cloned.1.call-update) | async-done | bytes 65552 | tf_op jit(solution)/shard_map/reduce_scatter | solution.py:158
  272.3 0.9 add_convert_fusion
  273.2 0.7 reshape.179
  (109 shorter events, 5.6 us)
Async XLA Ops:
  8.6 21.8 %all-to-all-start.1 = ((bf16[256,4,256]{0,2,1:T(8,128)(2,1)}), bf16[256,4,256]{0,2,1:T(8,128)(2,1)S(1)}, u32[]{:S(2)}, u32[]{:S(2)}) async-start(bf16[256,4,256]{0,2,1:T(8,128)(2,1)} %bitcast.2), calls=%async_computation.1 | async-start | bytes 1048576 | tf_op jit(solution)/shard_map/all_to_all | solution.py:118
  14.9 2.2 copy-start
  17.1 8.3 %copy-start.3 = (bf16[256,1024]{1,0:T(8,128)(2,1)S(1)}, bf16[256,1024]{1,0:T(8,128)(2,1)}, u32[]{:S(2)}) copy-start(bf16[256,1024]{1,0:T(8,128)(2,1)} %param.18) | copy-start | bytes 1572868
  17.1 20.6 %copy-start.2 = (bf16[4,4,8192]{2,1,0:T(4,128)(2,1)S(1)}, bf16[4,4,8192]{2,1,0:T(4,128)(2,1)}, u32[]{:S(2)}) copy-start(bf16[4,4,8192]{2,1,0:T(4,128)(2,1)} %param.14) | copy-start | bytes 786436
  17.1 20.7 %copy-start.4 = (f32[8192]{0:T(1024)S(1)}, f32[8192]{0:T(1024)}, u32[]{:S(2)}) copy-start(f32[8192]{0:T(1024)} %param.15) | copy-start | bytes 98308
  19.1 2.0 copy-start.1
  21.0 92.0 %collective-permute-start = (bf16[256,2048]{1,0:T(8,128)(2,1)}, bf16[256,2048]{1,0:T(8,128)(2,1)}, u32[]{:S(2)}, u32[]{:S(2)}) collective-permute-start(bf16[256,2048]{1,0:T(8,128)(2,1)} %get-tuple-element.199), channel_id=1, source_target_pairs={{0,1},{1,0},{2,3},{3,2},{4,5},{5,4},{6,7},{7,6},{8,9},{9,8},{10,11... | collective-permute-start | bytes 3145736 | tf_op jit(solution)/shard_map/ppermute | solution.py:106
  23.1 92.3 %collective-permute-start.1 = (bf16[256,2048]{1,0:T(8,128)(2,1)}, bf16[256,2048]{1,0:T(8,128)(2,1)}, u32[]{:S(2)}, u32[]{:S(2)}) collective-permute-start(bf16[256,2048]{1,0:T(8,128)(2,1)} %get-tuple-element.201), channel_id=1, source_target_pairs={{0,2},{1,3},{2,0},{3,1},{4,6},{5,7},{6,4},{7,5},{8,10},{9,11},{10,... | collective-permute-start | bytes 3145736 | tf_op jit(solution)/shard_map/ppermute | solution.py:106
  30.4 78.6 %all-to-all-start.2 = ((bf16[256,4,256]{0,2,1:T(8,128)(2,1)}), bf16[256,4,256]{0,2,1:T(8,128)(2,1)S(1)}, u32[]{:S(2)}, u32[]{:S(2)}) async-start(bf16[256,4,256]{0,2,1:T(8,128)(2,1)} %bitcast.5), calls=%async_computation.2 | async-start | bytes 1048576 | tf_op jit(solution)/shard_map/all_to_all | solution.py:119
  33.9 83.8 %collective-permute-start.2 = (bf16[256,2048]{1,0:T(8,128)(2,1)S(1)}, bf16[256,2048]{1,0:T(8,128)(2,1)}, u32[]{:S(2)}, u32[]{:S(2)}) collective-permute-start(bf16[256,2048]{1,0:T(8,128)(2,1)S(1)} %get-tuple-element.198), channel_id=1, source_target_pairs={{0,3},{1,2},{2,1},{3,0},{4,7},{5,6},{6,5},{7,4},{8,11},{9,10},{10,... | collective-permute-start | bytes 3145736 | tf_op jit(solution)/shard_map/ppermute | solution.py:106
  109.1 11.0 %all-to-all-start = ((bf16[16,8,1024]{2,0,1:T(8,128)(2,1)}), bf16[16,8,1024]{2,0,1:T(8,128)(2,1)S(1)}, u32[]{:S(2)}, u32[]{:S(2)}) async-start(bf16[16,8,1024]{2,0,1:T(8,128)(2,1)} %copy.44), calls=%async_computation | async-start | bytes 524288 | tf_op jit(solution)/shard_map/all_to_all | solution.py:128
  112.8 59.9 %reduce-scatter.3.cloned.1.call-start = ((), (), s32[]{:S(2)}) async-start(), calls=%async_computation.7 | async-start | bytes 1474560 | tf_op jit(solution)/shard_map/reduce_scatter | solution.py:129
  124.2 15.0 %copy-start.7 = (bf16[256]{0:T(256)(128)(2,1)S(1)}, bf16[256]{0:T(256)(128)(2,1)}, u32[]{:S(2)}) copy-start(bf16[256]{0:T(256)(128)(2,1)} %param.21) | copy-start | bytes 1540
  124.2 15.0 %copy-start.8 = (bf16[256]{0:T(256)(128)(2,1)S(1)}, bf16[256]{0:T(256)(128)(2,1)}, u32[]{:S(2)}) copy-start(bf16[256]{0:T(256)(128)(2,1)} %param.22) | copy-start | bytes 1540
  124.2 15.0 %copy-start.6 = (bf16[2048]{0:T(1024)(128)(2,1)S(1)}, bf16[2048]{0:T(1024)(128)(2,1)}, u32[]{:S(2)}) copy-start(bf16[2048]{0:T(1024)(128)(2,1)} %param.20) | copy-start | bytes 12292
  124.2 15.1 %copy-start.5 = (s32[4]{0:T(128)S(1)}, s32[4]{0:T(128)}, u32[]{:S(2)}) copy-start(s32[4]{0:T(128)} %param.25) | copy-start | bytes 52
  124.3 108.3 %all-to-all-start.3 = ((bf16[4,2048,256]{2,1,0:T(8,128)(2,1)}), bf16[4,2048,256]{2,1,0:T(8,128)(2,1)}, u32[]{:S(2)}, u32[]{:S(2)}) async-start(bf16[4,2048,256]{2,1,0:T(8,128)(2,1)} %bitcast.61), calls=%async_computation.4 | async-start | bytes 8388608 | tf_op jit(solution)/shard_map/all_to_all | solution.py:121
  139.2 133.1 %reduce-scatter.5.cloned.1.call-start = ((), (), s32[]{:S(2)}) async-start(), calls=%async_computation.8 | async-start | bytes 327680 | tf_op jit(solution)/shard_map/reduce_scatter | solution.py:158
Sparse Core Ops, SparseCore 0:
  124.3 48.3 reduce-scatter.2
  253.8 18.4 reduce-scatter.4
